TPU v7x, 32 devices: a whole 2x2x4 slice. The times are simulated.
32 devices in a mesh: dp: 8 (over y, x, core), tensor: 4 (over z).
Axes of the slice: x: 2, y: 2, z: 4, core: 2. Of those that a mesh axis runs over, the one named last changes fastest.
Arguments:
- tokens: bfloat16 [32, 256, 1152], P(('dp', 'tensor')), may hold values from -6 to 6
- timesteps: int32 [32], P('dp'), may hold values from 0 to 999
- labels: int32 [32], P('dp'), may hold values from 0 to 999
- item_counts: int32 [8], P('dp'), may hold values from 1 to 4
- cotangent: bfloat16 [32, 256, 1152], P(('dp', 'tensor')), may hold values from -6 to 6
- project_weight: bfloat16 [1152, 3, 1152], P(None, None, 'tensor'), may hold values from -0.1875 to 0.1875
- query_gain: bfloat16 [72], replicated, may hold values from 0.099609375 to 1.8984375
- key_gain: bfloat16 [72], replicated, may hold values from 0.099609375 to 1.8984375
- output_weight: bfloat16 [1152, 1152], P('tensor'), may hold values from -0.5 to 0.5
- output_bias: bfloat16 [1152], replicated, may hold values from -3 to 3
- expand_weight: bfloat16 [1152, 2, 3072], P(None, None, 'tensor'), may hold values from -0.1875 to 0.1875
- down_weight: bfloat16 [3072, 1152], P('tensor'), may hold values from -0.15625 to 0.15625
- down_bias: bfloat16 [1152], replicated, may hold values from -3 to 3
- modulate_weight: bfloat16 [1152, 6, 1152], P(None, None, 'tensor'), may hold values from -0.1875 to 0.1875
- modulate_bias: bfloat16 [6, 1152], P(None, 'tensor'), may hold values from -3 to 3
- time_weight: bfloat16 [256, 1152], replicated, may hold values from -0.5 to 0.5
- time_bias: bfloat16 [1152], replicated, may hold values from -3 to 3
- embed_weight: bfloat16 [1152, 1152], replicated, may hold values from -0.25 to 0.25
- embed_bias: bfloat16 [1152], replicated, may hold values from -3 to 3
- class_table: bfloat16 [1000, 1152], replicated, may hold values from -6 to 6
Outputs:
- result: bfloat16 [32, 256, 1152], P(('dp', 'tensor'))
- tokens_grad: bfloat16 [32, 256, 1152], P(('dp', 'tensor'))
- project_grad: float32 [1152, 3, 1152], P('dp', None, 'tensor')
- query_gain_grad: float32 [72], replicated
- key_gain_grad: float32 [72], replicated
- output_weight_grad: float32 [1152, 1152], P('tensor', 'dp')
- output_bias_grad: float32 [1152], replicated
- expand_grad: float32 [1152, 2, 3072], P('dp', None, 'tensor')
- down_grad: float32 [3072, 1152], P('tensor', 'dp')
- down_bias_grad: float32 [1152], replicated
- modulate_grad: float32 [1152, 6, 1152], P('dp', None, 'tensor')
- modulate_bias_grad: float32 [6, 1152], replicated
- time_grad: float32 [256, 1152], P(None, 'dp')
- time_bias_grad: float32 [1152], P('dp')
- embed_grad: float32 [1152, 1152], P('dp')
- embed_bias_grad: float32 [1152], P('dp')
- class_grad: float32 [1000, 1152], P(None, 'dp')
Inputs may be any that keep to these rules, and one draw needn't show every extreme that they name: `item_counts`: entry i counts the real items among the 4 items of index i of dp; they are its first ones.
All inputs are finite; a program needn't handle non-finite values.
Results may differ from a plain program's by a relative error of at most 0.03.
Values may be sent and summed in bfloat16 or wider, within the bound.
A program may use at most 256 MiB of HBM per device.

v0:
```python
import math
import jax
import jax.numpy as jnp
from jax import lax
from jax.sharding import PartitionSpec as P

HD = 72
FREQ = 256
GRID = 16
EPS = 1e-06


def layer_norm(value):
    center = value - jnp.mean(value, axis=-1, keepdims=True)
    inverse = lax.rsqrt(jnp.mean(center * center, axis=-1, keepdims=True) + EPS)
    return (center * inverse, inverse)


def layer_norm_back(normed, inverse, grad):
    return inverse * (
        grad
        - jnp.mean(grad, axis=-1, keepdims=True)
        - normed * jnp.mean(grad * normed, axis=-1, keepdims=True)
    )


def silu_slope(value):
    sigma = jax.nn.sigmoid(value)
    return sigma * (1.0 + value * (1.0 - sigma))


def rotate(value, positions):
    quarter = HD // 4
    rates = 10000.0 ** (-jnp.arange(quarter, dtype=jnp.float32) / quarter)
    places = ((positions // GRID).astype(jnp.float32), (positions % GRID).astype(jnp.float32))
    pieces = []
    for which_half in range(2):
        half_value = value[..., which_half * 2 * quarter : (which_half + 1) * 2 * quarter]
        angle = places[which_half][:, None] * rates[None, :]
        cosine = jnp.cos(angle)[None, :, None, :]
        sine = jnp.sin(angle)[None, :, None, :]
        first = half_value[..., :quarter]
        second = half_value[..., quarter:]
        pieces.append(first * cosine - second * sine)
        pieces.append(second * cosine + first * sine)
    return jnp.concatenate(pieces, axis=-1)


def head_prepare(raw, gain, positions):
    scaled = raw * lax.rsqrt(jnp.mean(raw * raw, axis=-1, keepdims=True) + EPS) * gain
    return rotate(scaled, positions)


def time_features(steps_in):
    half = FREQ // 2
    rates = jnp.exp(-math.log(10000.0) * jnp.arange(half, dtype=jnp.float32) / half)
    angle = steps_in.astype(jnp.float32)[:, None] * rates[None, :]
    return jnp.concatenate([jnp.cos(angle), jnp.sin(angle)], axis=-1)


def shards(
    tokens,
    timesteps,
    labels,
    item_counts,
    cotangent,
    project_weight,
    query_gain,
    key_gain,
    output_weight,
    output_bias,
    expand_weight,
    down_weight,
    down_bias,
    modulate_weight,
    modulate_bias,
    time_weight,
    time_bias,
    embed_weight,
    embed_bias,
    class_table,
):
    local_items, length, width = tokens.shape
    items = timesteps.shape[0]
    slab = modulate_weight.shape[2]
    heads_here = project_weight.shape[2] // HD
    scale = HD ** (-0.5)
    lane = lax.axis_index("tensor")
    first_item = lane * local_items
    live = (first_item + jnp.arange(local_items) < item_counts[0]).astype(jnp.float32)[
        :, None, None
    ]
    index = lax.axis_index("dp")
    tags = lax.all_gather(jnp.stack([timesteps, labels]), "dp", axis=1, tiled=True)
    time_feat = time_features(tags[0]).astype(jnp.bfloat16)
    pre_hidden = jnp.dot(
        time_feat, time_weight, preferred_element_type=jnp.float32
    ) + time_bias.astype(jnp.float32)
    time_hidden = jax.nn.silu(pre_hidden).astype(jnp.bfloat16)
    condition = (
        jnp.dot(time_hidden, embed_weight, preferred_element_type=jnp.float32)
        + embed_bias.astype(jnp.float32)
        + jnp.take(class_table, tags[1], axis=0).astype(jnp.float32)
    )
    cond_act = jax.nn.silu(condition).astype(jnp.bfloat16)
    cond_act_here = lax.dynamic_slice_in_dim(cond_act, index * items, items, 0)
    condition_here = lax.dynamic_slice_in_dim(condition, index * items, items, 0)
    modulation_part = (
        jnp.einsum(
            "bd,dke->bke", cond_act_here, modulate_weight, preferred_element_type=jnp.float32
        )
        + modulate_bias.astype(jnp.float32)
    ).astype(jnp.bfloat16)
    modulation_local = lax.all_to_all(
        modulation_part, "tensor", split_axis=0, concat_axis=2, tiled=True
    ).astype(jnp.float32)
    local_parts = [modulation_local[:, which][:, None, :] for which in range(6)]
    attend_shift, attend_scale, attend_gate, feed_shift, feed_scale, feed_gate = local_parts
    positions = jnp.arange(length)
    token_local = tokens.astype(jnp.float32)
    normed_local, inverse_local = layer_norm(token_local)
    mod_in = lax.all_gather(
        (normed_local * (1.0 + attend_scale) + attend_shift).astype(jnp.bfloat16),
        "tensor",
        axis=0,
        tiled=True,
    )
    projected = jnp.einsum(
        "bld,dke->blke", mod_in, project_weight, preferred_element_type=jnp.float32
    )
    split = projected.reshape(items, length, 3, heads_here, HD)
    query_gain_f = query_gain.astype(jnp.float32)
    key_gain_f = key_gain.astype(jnp.float32)
    queries = head_prepare(split[:, :, 0], query_gain_f, positions).astype(jnp.bfloat16)
    keys = head_prepare(split[:, :, 1], key_gain_f, positions).astype(jnp.bfloat16)
    values = split[:, :, 2].astype(jnp.bfloat16)
    scores = (
        jnp.einsum("bqhd,bkhd->bhqk", queries, keys, preferred_element_type=jnp.float32) * scale
    )
    top = jnp.max(scores, axis=-1, keepdims=True)
    logsum = top + jnp.log(jnp.sum(jnp.exp(scores - top), axis=-1, keepdims=True))
    probs = jnp.exp(scores - logsum).astype(jnp.bfloat16)
    mixed = jnp.einsum("bhqk,bkhd->bqhd", probs, values, preferred_element_type=jnp.float32)
    mixed = mixed.reshape(items, length, heads_here * HD).astype(jnp.bfloat16)
    piece = mixed
    attend_branch = lax.psum_scatter(
        jnp.einsum("blh,hd->bld", piece, output_weight, preferred_element_type=jnp.float32).astype(
            jnp.bfloat16
        ),
        "tensor",
        scatter_dimension=0,
        tiled=True,
    ).astype(jnp.float32) + output_bias.astype(jnp.float32)
    residual = token_local + attend_gate * attend_branch
    normed_two, inverse_two = layer_norm(residual)
    mod_two = (normed_two * (1.0 + feed_scale) + feed_shift).astype(jnp.bfloat16)
    mod_two_all = lax.all_gather(mod_two, "tensor", axis=0, tiled=True)
    gate_up = jnp.einsum(
        "bld,dkf->blkf", mod_two_all, expand_weight, preferred_element_type=jnp.float32
    )
    gate = gate_up[:, :, 0]
    upper = gate_up[:, :, 1]
    hidden = (jax.nn.silu(gate) * upper).astype(jnp.bfloat16)
    piece = hidden
    feed_branch = lax.psum_scatter(
        jnp.einsum("blf,fd->bld", piece, down_weight, preferred_element_type=jnp.float32).astype(
            jnp.bfloat16
        ),
        "tensor",
        scatter_dimension=0,
        tiled=True,
    ).astype(jnp.float32) + down_bias.astype(jnp.float32)
    result = (live * (residual + feed_gate * feed_branch)).astype(jnp.bfloat16)
    out_grad = cotangent.astype(jnp.float32) * live
    branch_grad = (out_grad * feed_gate).astype(jnp.bfloat16)
    down_bias_part = jnp.sum(branch_grad.astype(jnp.float32), axis=(0, 1))
    piece = lax.all_gather(branch_grad, "tensor", axis=0, tiled=True)
    weight_total = jnp.einsum("blf,bld->fd", hidden, piece, preferred_element_type=jnp.float32)
    rows_grad = jnp.einsum("bld,fd->blf", piece, down_weight, preferred_element_type=jnp.float32)
    hidden_total = rows_grad
    down_grad = weight_total
    gate_up_grad = jnp.stack(
        [hidden_total * upper * silu_slope(gate), hidden_total * jax.nn.silu(gate)], axis=2
    ).astype(jnp.bfloat16)
    expand_grad = jnp.einsum(
        "bld,blkf->dkf", mod_two_all, gate_up_grad, preferred_element_type=jnp.float32
    )
    piece = gate_up_grad
    mod_two_grad = lax.psum_scatter(
        jnp.einsum(
            "blkf,dkf->bld", piece, expand_weight, preferred_element_type=jnp.float32
        ).astype(jnp.bfloat16),
        "tensor",
        scatter_dimension=0,
        tiled=True,
    ).astype(jnp.float32)
    residual_grad = out_grad + layer_norm_back(
        normed_two, inverse_two, mod_two_grad * (1.0 + feed_scale)
    )
    attend_grad = (residual_grad * attend_gate).astype(jnp.bfloat16)
    output_bias_part = jnp.sum(attend_grad.astype(jnp.float32), axis=(0, 1))
    piece = lax.all_gather(attend_grad, "tensor", axis=0, tiled=True)
    weight_total = jnp.einsum("blh,bld->hd", mixed, piece, preferred_element_type=jnp.float32)
    rows_grad = jnp.einsum("bld,hd->blh", piece, output_weight, preferred_element_type=jnp.float32)
    output_weight_grad = weight_total
    mixed_grad = rows_grad
    mixed_grad = mixed_grad.reshape(items, length, heads_here, HD).astype(jnp.bfloat16)
    again = jnp.einsum("bqhd,bkhd->bhqk", queries, keys, preferred_element_type=jnp.float32) * scale
    prob_float = jnp.exp(again - logsum)
    prob_low = prob_float.astype(jnp.bfloat16)
    prob_grad = jnp.einsum(
        "bqhd,bkhd->bhqk", mixed_grad, values, preferred_element_type=jnp.float32
    )
    score_grad = (
        prob_float * (prob_grad - jnp.sum(prob_float * prob_grad, axis=-1, keepdims=True))
    ).astype(jnp.bfloat16)
    query_grad = (
        jnp.einsum("bhqk,bkhd->bqhd", score_grad, keys, preferred_element_type=jnp.float32) * scale
    )
    key_grad = (
        jnp.einsum("bhqk,bqhd->bkhd", score_grad, queries, preferred_element_type=jnp.float32)
        * scale
    )
    value_grad = jnp.einsum(
        "bhqk,bqhd->bkhd", prob_low, mixed_grad, preferred_element_type=jnp.float32
    )

    def prepare_here(raw, gain):
        return head_prepare(raw, gain, positions)

    _, query_back = jax.vjp(prepare_here, split[:, :, 0], query_gain_f)
    raw_query_grad, query_gain_part = query_back(query_grad)
    _, key_back = jax.vjp(prepare_here, split[:, :, 1], key_gain_f)
    raw_key_grad, key_gain_part = key_back(key_grad)
    projected_grad = jnp.stack([raw_query_grad, raw_key_grad, value_grad], axis=2)
    projected_grad = projected_grad.reshape(items, length, 3, heads_here * HD).astype(jnp.bfloat16)
    project_grad = jnp.einsum(
        "bld,blke->dke", mod_in, projected_grad, preferred_element_type=jnp.float32
    )
    piece = projected_grad
    mod_in_grad = lax.psum_scatter(
        jnp.einsum(
            "blke,dke->bld", piece, project_weight, preferred_element_type=jnp.float32
        ).astype(jnp.bfloat16),
        "tensor",
        scatter_dimension=0,
        tiled=True,
    ).astype(jnp.float32)
    tokens_grad = (
        residual_grad
        + layer_norm_back(normed_local, inverse_local, mod_in_grad * (1.0 + attend_scale))
    ).astype(jnp.bfloat16)
    modulation_grad_part = jnp.stack(
        [
            jnp.sum(mod_in_grad, axis=1),
            jnp.sum(mod_in_grad * normed_local, axis=1),
            jnp.sum(residual_grad * attend_branch, axis=1),
            jnp.sum(mod_two_grad, axis=1),
            jnp.sum(mod_two_grad * normed_two, axis=1),
            jnp.sum(out_grad * feed_branch, axis=1),
        ],
        axis=1,
    )
    modulation_grad = lax.all_to_all(
        modulation_grad_part, "tensor", split_axis=2, concat_axis=0, tiled=True
    ).astype(jnp.bfloat16)
    modulate_bias_part = jnp.sum(modulation_grad.astype(jnp.float32), axis=0)
    cond_part = jnp.einsum(
        "bke,dke->bd", modulation_grad, modulate_weight, preferred_element_type=jnp.float32
    )
    cond_total = lax.psum(cond_part, "tensor")
    cond_grad_here = (cond_total * silu_slope(condition_here)).astype(jnp.bfloat16)
    packed = jnp.concatenate([cond_grad_here, modulation_grad.reshape(items, 6 * slab)], axis=1)
    packed = lax.all_gather(packed, "dp", axis=0, tiled=True)
    cond_grad = packed[:, :width]
    modulation_grad_all = packed[:, width:].reshape(-1, 6, slab)
    share = width // lax.axis_size("dp")

    def mine(value, axis):
        return lax.dynamic_slice_in_dim(value, index * share, share, axis)

    one_hot = (tags[1][:, None] == jnp.arange(class_table.shape[0])[None, :]).astype(jnp.bfloat16)
    cond_grad_mine = mine(cond_grad, 1)
    class_grad = jnp.einsum(
        "bc,bd->cd", one_hot, cond_grad_mine, preferred_element_type=jnp.float32
    )
    pre_grad = (
        jnp.einsum(
            "be,de->bd", cond_grad, mine(embed_weight, 0), preferred_element_type=jnp.float32
        )
        * silu_slope(mine(pre_hidden, 1))
    ).astype(jnp.bfloat16)
    modulate_grad = jnp.einsum(
        "bd,bke->dke", mine(cond_act, 1), modulation_grad_all, preferred_element_type=jnp.float32
    )
    embed_grad = jnp.einsum(
        "bd,be->de", mine(time_hidden, 1), cond_grad, preferred_element_type=jnp.float32
    )
    embed_bias_grad = jnp.sum(cond_grad_mine.astype(jnp.float32), axis=0)
    time_grad = jnp.einsum("bf,bd->fd", time_feat, pre_grad, preferred_element_type=jnp.float32)
    time_bias_grad = jnp.sum(pre_grad.astype(jnp.float32), axis=0)
    bias_wide = lax.dynamic_update_slice_in_dim(
        jnp.zeros((6, width), jnp.float32), modulate_bias_part, lane * slab, 1
    )
    small = jnp.concatenate(
        [output_bias_part, down_bias_part, bias_wide.reshape(-1), query_gain_part, key_gain_part]
    )
    small = lax.psum(small, ("dp", "tensor"))
    output_bias_grad = small[:width]
    down_bias_grad = small[width : 2 * width]
    modulate_bias_grad = small[2 * width : 8 * width].reshape(6, width)
    query_gain_grad = small[8 * width : 8 * width + HD]
    key_gain_grad = small[8 * width + HD :]

    def scatter(value, axis):
        value = value.astype(jnp.bfloat16)
        return lax.psum_scatter(value, "dp", scatter_dimension=axis, tiled=True).astype(jnp.float32)

    project_grad = scatter(project_grad, 0)
    output_weight_grad = scatter(output_weight_grad, 1)
    expand_grad = scatter(expand_grad, 0)
    down_grad = scatter(down_grad, 1)
    return (
        result,
        tokens_grad,
        project_grad,
        query_gain_grad,
        key_gain_grad,
        output_weight_grad,
        output_bias_grad,
        expand_grad,
        down_grad,
        down_bias_grad,
        modulate_grad,
        modulate_bias_grad,
        time_grad,
        time_bias_grad,
        embed_grad,
        embed_bias_grad,
        class_grad,
    )


def solution(mesh):
    return jax.shard_map(
        shards,
        mesh=mesh,
        in_specs=(
            P(("dp", "tensor"), None, None),
            P("dp"),
            P("dp"),
            P("dp"),
            P(("dp", "tensor"), None, None),
            P(None, None, "tensor"),
            P(),
            P(),
            P("tensor", None),
            P(),
            P(None, None, "tensor"),
            P("tensor", None),
            P(),
            P(None, None, "tensor"),
            P(None, "tensor"),
            P(),
            P(),
            P(),
            P(),
            P(),
        ),
        out_specs=(
            P(("dp", "tensor"), None, None),
            P(("dp", "tensor"), None, None),
            P("dp", None, "tensor"),
            P(),
            P(),
            P("tensor", "dp"),
            P(),
            P("dp", None, "tensor"),
            P("tensor", "dp"),
            P(),
            P("dp", None, "tensor"),
            P(),
            P(None, "dp"),
            P("dp"),
            P("dp", None),
            P("dp"),
            P(None, "dp"),
        ),
        check_vma=False,
    )
```

profile of v0, /device:TPU:0, one launch (start us, length us, event | category | flops | bytes accessed | tf_op | source)
XLA Modules:
  0.0 764.2 jit_solution(1192706459011180409)
XLA Ops:
  8.1 10.4 %all-gather = s32[8,4,2]{1,2,0:T(2,128)S(1)} all-gather(s32[1,4,2]{1,2,0:T(2,128)S(1)} %add_bitcast_fusion), channel_id=1, replica_groups=mesh['dp'=8,'tensor'=4] {'dp'}, dimensions={0}, use_global_device_ids=true | all-gather | bytes 288 | tf_op jit(solution)/shard_map/all_gather | solution.py:94
  29.4 4.9 all-to-all-start
  34.8 5.1 all-to-all-done
  42.8 47.1 %all-gather.7.cloned.1.call-done = bf16[4,256,1152]{2,1,0:T(8,128)(2,1)} async-done(((bf16[1,256,1152]{2,1,0:T(8,128)(2,1)}), bf16[4,256,1152]{2,1,0:T(8,128)(2,1)}) %all-gather.7.cloned.1.call-update) | async-done | bytes 2359312 | tf_op jit(solution)/shard_map/all_gather | solution.py:122
  90.0 4.7 fusion.10
  107.8 45.3 %reduce-scatter.9.cloned.1.call-done = bf16[1,256,1152]{2,1,0:T(8,128)(2,1)} async-done(((bf16[4,256,1152]{2,1,0:T(8,128)(2,1)}), bf16[1,256,1152]{2,1,0:T(8,128)(2,1)}) %reduce-scatter.9.cloned.1.call-update) | async-done | bytes 589840 | tf_op jit(solution)/shard_map/reduce_scatter | solution.py:146
  160.6 45.8 %all-gather.9.cloned.1.call-done = bf16[4,256,1152]{2,1,0:T(8,128)(2,1)} async-done(((bf16[1,256,1152]{2,1,0:T(8,128)(2,1)}), bf16[4,256,1152]{2,1,0:T(8,128)(2,1)}) %all-gather.9.cloned.1.call-update) | async-done | bytes 2359312 | tf_op jit(solution)/shard_map/all_gather | solution.py:157
  206.4 9.6 %fusion.1 = f32[4,256,2,768]{3,1,2,0:T(8,128)} fusion(bf16[1152,2,768]{2,1,0:T(2,128)(2,1)} %param.30, bf16[4,256,1152]{2,1,0:T(8,128)(2,1)} %all-gather.9.cloned.1.call-done), kind=kOutput, calls=%fused_computation.14 | convolution fusion | flops 3623878656 | bytes 12189696 | tf_op jit(solution)/shard_map/bld,dkf->blkf/dot_general | solution.py:158
  216.0 41.2 %all-gather.11.cloned.1.call-done = bf16[4,256,1152]{2,1,0:T(8,128)(2,1)} async-done(((bf16[1,256,1152]{2,1,0:T(8,128)(2,1)}), bf16[4,256,1152]{2,1,0:T(8,128)(2,1)}) %all-gather.11.cloned.1.call-update) | async-done | bytes 2359312 | tf_op jit(solution)/shard_map/all_gather | solution.py:177
  257.2 8.4 %fusion.26 = (bf16[4,256,1,768]{3,1,0,2:T(8,128)(2,1)S(1)}, bf16[4,256,1,768]{3,1,0,2:T(8,128)(2,1)S(1)}, bf16[4,256,768]{2,1,0:T(8,128)(2,1)}) fusion(f32[4,256,2,768]{3,1,2,0:T(8,128)} %fusion.1, bf16[4,256,1152]{2,1,0:T(8,128)(2,1)} %all-gather.11.cloned.1.call-done, bf16[768,1152]{1,0:T(8,128)(2,1)} %param.31), kind=kOutput, calls=%fused_computation.62 | convolution fusion | flops 1823735808 | bytes 15138816 | tf_op jit(solution)/shard_map/bld,fd->blf/dot_general | solution.py:179
  267.2 5.6 bitcast_convert_fusion.3
  272.8 5.6 convolution_convert_fusion
  279.8 39.6 %reduce-scatter.13.cloned.1.call-done = bf16[1,256,1152]{2,1,0:T(8,128)(2,1)} async-done(((bf16[4,256,1152]{2,1,0:T(8,128)(2,1)}), bf16[1,256,1152]{2,1,0:T(8,128)(2,1)}) %reduce-scatter.13.cloned.1.call-update) | async-done | bytes 589840 | tf_op jit(solution)/shard_map/reduce_scatter | solution.py:189
  323.2 45.5 %reduce-scatter.11.cloned.1.call-done = bf16[1,256,1152]{2,1,0:T(8,128)(2,1)} async-done(((bf16[4,256,1152]{2,1,0:T(8,128)(2,1)}), bf16[1,256,1152]{2,1,0:T(8,128)(2,1)}) %reduce-scatter.11.cloned.1.call-update) | async-done | bytes 589840 | tf_op jit(solution)/shard_map/reduce_scatter | solution.py:165
  368.7 4.1 multiply_reduce_fusion.5
  375.4 11.2 %reduce-scatter.23.cloned.1.call-start = ((), (), s32[]{:S(2)}) async-start(), calls=%async_computation.21 | async-start | bytes 1990656 | tf_op jit(solution)/shard_map/reduce_scatter | solution.py:317
  386.6 5.4 fusion.4
  392.1 8.2 %bitcast_convert_fusion = bf16[1152,2,768]{2,0,1:T(8,128)(2,1)} fusion(bf16[4,256,1152]{2,1,0:T(8,128)(2,1)} %all-gather.9.cloned.1.call-done, bf16[4,256,1,768]{3,1,0,2:T(8,128)(2,1)} %copy-done.82, bf16[4,256,1,768]{3,1,0,2:T(8,128)(2,1)} %copy-done.81), kind=kOutput, calls=%fused_computation.1 | convolution fusion | flops 3631939584 | bytes 9043968 | tf_op jit(solution)/shard_map/bld,blkf->dkf/dot_general | solution.py:185
  400.4 24.6 %all-gather.13.cloned.1.call-done = bf16[4,256,1152]{2,1,0:T(8,128)(2,1)} async-done(((bf16[1,256,1152]{2,1,0:T(8,128)(2,1)}), bf16[4,256,1152]{2,1,0:T(8,128)(2,1)}) %all-gather.13.cloned.1.call-update) | async-done | bytes 2359312 | tf_op jit(solution)/shard_map/all_gather | solution.py:202
  445.4 3.5 convolution_convert_fusion.2
  449.8 5.3 bitcast_convert_fusion.1
  455.4 6.5 bitcast_convert_fusion.2
  461.9 4.4 reduce-scatter.23.cloned.1.call-done
  468.1 49.6 %reduce-scatter.21.cloned.1.call-done = bf16[144,2,768]{2,0,1:T(8,128)(2,1)} async-done(((bf16[1152,2,768]{2,0,1:T(8,128)(2,1)}), bf16[144,2,768]{2,0,1:T(8,128)(2,1)}) %reduce-scatter.21.cloned.1.call-update) | async-done | bytes 442384 | tf_op jit(solution)/shard_map/reduce_scatter | solution.py:317
  520.0 35.5 %reduce-scatter.19.cloned.1.call-done = bf16[288,144]{0,1:T(8,128)(2,1)} async-done(((bf16[288,1152]{0,1:T(8,128)(2,1)}), bf16[288,144]{0,1:T(8,128)(2,1)}) %reduce-scatter.19.cloned.1.call-update) | async-done | bytes 82960 | tf_op jit(solution)/shard_map/reduce_scatter | solution.py:317
  557.0 44.9 %reduce-scatter.17.cloned.1.call-done = bf16[144,3,288]{2,0,1:T(8,128)(2,1)} async-done(((bf16[1152,3,288]{2,0,1:T(8,128)(2,1)}), bf16[144,3,288]{2,0,1:T(8,128)(2,1)}) %reduce-scatter.17.cloned.1.call-update) | async-done | bytes 248848 | tf_op jit(solution)/shard_map/reduce_scatter | solution.py:317
  603.8 48.0 %reduce-scatter.15.cloned.1.call-done = bf16[1,256,1152]{2,1,0:T(8,128)(2,1)} async-done(((bf16[4,256,1152]{2,1,0:T(8,128)(2,1)}), bf16[1,256,1152]{2,1,0:T(8,128)(2,1)}) %reduce-scatter.15.cloned.1.call-update) | async-done | bytes 589840 | tf_op jit(solution)/shard_map/reduce_scatter | solution.py:241
  656.5 7.7 %reduce.26 = bf16[1152,6]{1,0:T(8,128)(2,1)S(1)} reduce(bf16[1152,1,6]{2,1,0:T(2,128)(2,1)} %bitcast.210, bf16[]{:T(256)} %broadcast.432), dimensions={1}, to_apply=%bitcast.178.reduce_sub_computation | reduce | bytes 27650
  665.2 3.3 all-to-all-start.1
  675.8 39.6 %psum.14 = f32[9360]{0:T(1024)S(1)} all-reduce(f32[9360]{0:T(1024)S(1)} %concatenate.23), channel_id=1, replica_groups=mesh['dp'=8,'tensor'=4] {'dp','tensor'}, use_global_device_ids=true, to_apply=%region_31.32 | all-reduce | flops 9360 | bytes 74880 | tf_op jit(solution)/shard_map/psum | solution.py:308
  719.4 17.1 %psum.15 = f32[4,1152]{1,0:T(4,128)S(1)} all-reduce(f32[4,1152]{1,0:T(4,128)S(1)} %convolution_bitcast_fusion.2), channel_id=1, replica_groups=mesh['dp'=8,'tensor'=4] {'tensor'}, use_global_device_ids=true, to_apply=%region_35.36 | all-reduce | flops 4608 | bytes 36864 | tf_op jit(solution)/shard_map/psum | solution.py:271
  737.5 10.0 %all-gather.1 = bf16[8,4,2880]{2,1,0:T(4,128)(2,1)S(1)} all-gather(bf16[1,4,2880]{2,1,0:T(4,128)(2,1)S(1)} %maximum_bitcast_fusion), channel_id=1, replica_groups=mesh['dp'=8,'tensor'=4] {'dp'}, dimensions={0}, use_global_device_ids=true | all-gather | bytes 207360 | tf_op jit(solution)/shard_map/all_gather | solution.py:274
  (309 shorter events, 100.1 us)
Async XLA Ops:
  7.2 19.0 %copy-start = (bf16[1152,1152]{1,0:T(8,128)(2,1)S(1)}, bf16[1152,1152]{1,0:T(8,128)(2,1)}, u32[]{:S(2)}) copy-start(bf16[1152,1152]{1,0:T(8,128)(2,1)} %param.37) | copy-start | bytes 7962628
  21.4 6.0 copy-start.54
  21.4 6.0 copy-start.56
  27.4 6.9 copy-start.3
  29.4 10.5 %all-to-all-start = ((bf16[4,6,288]{2,1,0:T(8,128)(2,1)}), bf16[4,6,288]{2,1,0:T(8,128)(2,1)S(1)}, u32[]{:S(2)}, u32[]{:S(2)}) async-start(bf16[4,6,288]{2,1,0:T(8,128)(2,1)} %copy.133), calls=%async_computation | async-start | bytes 49152 | tf_op jit(solution)/shard_map/all_to_all | solution.py:114
  34.3 55.7 %all-gather.7.cloned.1.call-start = ((), (), s32[]{:S(2)}) async-start(), calls=%async_computation.10 | async-start | bytes 2949120 | tf_op jit(solution)/shard_map/all_gather | solution.py:122
  34.4 8.0 %copy-start.58 = (f32[256]{0:T(256)}, f32[256]{0:T(256)S(1)}, u32[]{:S(2)}) copy-start(f32[256]{0:T(256)S(1)} %broadcast_multiply_fusion.5) | copy-start | bytes 3076
  34.8 7.7 %copy-start.79 = (bf16[72]{0:T(256)(128)(2,1)S(1)}, bf16[72]{0:T(256)(128)(2,1)}, u32[]{:S(2)}) copy-start(bf16[72]{0:T(256)(128)(2,1)} %param.26) | copy-start | bytes 436
  34.8 7.7 %copy-start.80 = (bf16[72]{0:T(256)(128)(2,1)S(1)}, bf16[72]{0:T(256)(128)(2,1)}, u32[]{:S(2)}) copy-start(bf16[72]{0:T(256)(128)(2,1)} %param.27) | copy-start | bytes 436
  34.8 59.9 %copy-start.61 = (f32[256]{0:T(256)}, f32[256]{0:T(256)S(1)}, u32[]{:S(2)}) copy-start(f32[256]{0:T(256)S(1)} %add_rsqrt_fusion.1) | copy-start | bytes 3076
  42.4 110.7 %reduce-scatter.9.cloned.1.call-start = ((), (), s32[]{:S(2)}) async-start(), calls=%async_computation.11 | async-start | bytes 2949120 | tf_op jit(solution)/shard_map/reduce_scatter | solution.py:146
  42.5 52.8 %copy-start.68 = (f32[72]{0:T(128)}, f32[72]{0:T(128)S(1)}, u32[]{:S(2)}) copy-start(f32[72]{0:T(128)S(1)} %convert_element_type.306) | copy-start | bytes 868
  42.5 53.9 %copy-start.70 = (f32[72]{0:T(128)}, f32[72]{0:T(128)S(1)}, u32[]{:S(2)}) copy-start(f32[72]{0:T(128)S(1)} %convert_element_type.309) | copy-start | bytes 868
  106.5 99.9 %all-gather.9.cloned.1.call-start = ((), (), s32[]{:S(2)}) async-start(), calls=%async_computation.12 | async-start | bytes 2949120 | tf_op jit(solution)/shard_map/all_gather | solution.py:157
  156.9 100.3 %all-gather.11.cloned.1.call-start = ((), (), s32[]{:S(2)}) async-start(), calls=%async_computation.14 | async-start | bytes 2949120 | tf_op jit(solution)/shard_map/all_gather | solution.py:177
  160.3 159.2 %reduce-scatter.13.cloned.1.call-start = ((), (), s32[]{:S(2)}) async-start(), calls=%async_computation.15 | async-start | bytes 2949120 | tf_op jit(solution)/shard_map/reduce_scatter | solution.py:189
  257.2 10.0 %copy-start.75 = (bf16[1152,2,768]{2,1,0:T(2,128)(2,1)S(1)}, bf16[1152,2,768]{2,1,0:T(2,128)(2,1)}, u32[]{:S(2)}) copy-start(bf16[1152,2,768]{2,1,0:T(2,128)(2,1)} %param.30) | copy-start | bytes 10616836
  272.8 95.9 %reduce-scatter.11.cloned.1.call-start = ((), (), s32[]{:S(2)}) async-start(), calls=%async_computation.13 | async-start | bytes 2949120 | tf_op jit(solution)/shard_map/reduce_scatter | solution.py:165
  278.5 146.5 %all-gather.13.cloned.1.call-start = ((), (), s32[]{:S(2)}) async-start(), calls=%async_computation.16 | async-start | bytes 2949120 | tf_op jit(solution)/shard_map/all_gather | solution.py:202
  375.4 90.9 %reduce-scatter.23.cloned.1.call-start = ((), (), s32[]{:S(2)}) async-start(), calls=%async_computation.21 | async-start | bytes 1990656 | tf_op jit(solution)/shard_map/reduce_scatter | solution.py:317
  392.0 125.7 %reduce-scatter.21.cloned.1.call-start = ((), (), s32[]{:S(2)}) async-start(), calls=%async_computation.20 | async-start | bytes 3981312 | tf_op jit(solution)/shard_map/reduce_scatter | solution.py:317
  400.3 155.1 %reduce-scatter.19.cloned.1.call-start = ((), (), s32[]{:S(2)}) async-start(), calls=%async_computation.19 | async-start | bytes 995328 | tf_op jit(solution)/shard_map/reduce_scatter | solution.py:317
  443.3 158.7 %reduce-scatter.17.cloned.1.call-start = ((), (), s32[]{:S(2)}) async-start(), calls=%async_computation.18 | async-start | bytes 2985984 | tf_op jit(solution)/shard_map/reduce_scatter | solution.py:317
  455.1 196.7 %reduce-scatter.15.cloned.1.call-start = ((), (), s32[]{:S(2)}) async-start(), calls=%async_computation.17 | async-start | bytes 2949120 | tf_op jit(solution)/shard_map/reduce_scatter | solution.py:241
  461.9 6.2 copy-start.64
  461.9 6.2 copy-start.63
  461.9 6.2 copy-start.67
  461.9 6.2 copy-start.66
  468.1 183.7 %copy-start.48 = (f32[1152]{0:T(1024)S(1)}, f32[1152]{0:T(1024)}, u32[]{:S(2)}) copy-start(f32[1152]{0:T(1024)} %copy-done.47) | copy-start | bytes 13828
  468.1 183.7 %copy-start.59 = (f32[256]{0:T(256)S(1)}, f32[256]{0:T(256)}, u32[]{:S(2)}) copy-start(f32[256]{0:T(256)} %copy-done.58) | copy-start | bytes 3076
  468.1 183.7 %copy-start.62 = (f32[256]{0:T(256)S(1)}, f32[256]{0:T(256)}, u32[]{:S(2)}) copy-start(f32[256]{0:T(256)} %copy-done.61) | copy-start | bytes 3076
  665.2 8.8 %all-to-all-start.1 = ((bf16[4,2,864]{2,1,0:T(2,128)(2,1)}), bf16[4,2,864]{2,1,0:T(2,128)(2,1)S(1)}, u32[]{:S(2)}, u32[]{:S(2)}) async-start(bf16[4,2,864]{2,1,0:T(2,128)(2,1)} %reshape.475), calls=%async_computation.6 | async-start | bytes 28672 | tf_op jit(solution)/shard_map/all_to_all | solution.py:264
  (65 other events, 135.1 us)
Sparse Core Ops, SparseCore 0:
  42.5 47.3 all-gather.6
  106.6 46.4 reduce-scatter.8
  157.0 49.3 all-gather.8
  208.4 48.7 all-gather.10
  272.9 46.4 reduce-scatter.12
  321.6 47.0 reduce-scatter.10
  375.5 49.3 all-gather.12
  428.3 37.9 reduce-scatter.22
  469.8 47.8 reduce-scatter.20
  520.8 34.6 reduce-scatter.18
  558.9 42.9 reduce-scatter.16
  604.1 47.6 reduce-scatter.14
where the time goes:
time: 774 us; the launch traced here: 764 us
  waiting for transfers between devices  480 us (62%)
  matrix products  92 us (12%)
  blocking collectives  77.2 us (10%)
  other arithmetic  53.3 us (7%)
  local copies, waits for them, and re-layouts  25.5 us (3%)
  starting transfers between devices  20.2 us (3%)
  between operations  16.4 us (2%)
    reduce_scatter x4, waiting for transfers between devices, scatter(): lax.psum_scatter(value, 'dp', scatter_dimension=axis, tiled=True)  134 us
    reduce_scatter x1, waiting for transfers between devices, shards(): lax.psum_scatter(jnp.einsum('blke,dke->bld', piece, project_weight, prefe...  48 us
    all_gather x1, waiting for transfers between devices, shards(): lax.all_gather((normed_local * (1.0 + attend_scale) + attend_shift).astyp...  47.1 us
    all_gather x1, waiting for transfers between devices, shards(): mod_two_all = lax.all_gather(mod_two, 'tensor', axis=0, tiled=True)  45.8 us
    reduce_scatter x1, waiting for transfers between devices, shards(): lax.psum_scatter(jnp.einsum('blf,fd->bld', piece, down_weight, preferred_...  45.5 us
    reduce_scatter x1, waiting for transfers between devices, shards(): lax.psum_scatter(jnp.einsum('blh,hd->bld', piece, output_weight, preferre...  45.3 us
    all_gather x1, waiting for transfers between devices, shards(): piece = lax.all_gather(branch_grad, 'tensor', axis=0, tiled=True)  41.2 us
    psum x1, blocking collectives, shards(): small = lax.psum(small, ('dp', 'tensor'))  39.6 us
  transfers between devices with their start and end apart: 14, of which 14 were waited for; matrix products, arithmetic and copies ran while one was open for 11% of the time, Pallas kernels for 0%

commit v1 on v0

--- a/solution.py
+++ b/solution.py
@@ -8,6 +8,24 @@
 FREQ = 256
 GRID = 16
 EPS = 1e-06
+
+
+def ring_gather(array, axis, dim):
+    ways, here, step = (lax.axis_size(axis), lax.axis_index(axis), array.shape[dim])
+    shape = [n * ways if d == dim else n for d, n in enumerate(array.shape)]
+    full = lax.dynamic_update_slice_in_dim(
+        jnp.zeros(shape, array.dtype), array, here * step, axis=dim
+    )
+    going_up = going_down = array
+    for far in range(1, ways // 2 + 1):
+        going_up = lax.ppermute(going_up, axis, [(d, (d + 1) % ways) for d in range(ways)])
+        full = lax.dynamic_update_slice_in_dim(full, going_up, (here - far) % ways * step, axis=dim)
+        if 2 * far < ways:
+            going_down = lax.ppermute(going_down, axis, [(d, (d - 1) % ways) for d in range(ways)])
+            full = lax.dynamic_update_slice_in_dim(
+                full, going_down, (here + far) % ways * step, axis=dim
+            )
+    return full
 
 
 def layer_norm(value):
@@ -199,7 +217,7 @@
     )
     attend_grad = (residual_grad * attend_gate).astype(jnp.bfloat16)
     output_bias_part = jnp.sum(attend_grad.astype(jnp.float32), axis=(0, 1))
-    piece = lax.all_gather(attend_grad, "tensor", axis=0, tiled=True)
+    piece = ring_gather(attend_grad, "tensor", 0)
     weight_total = jnp.einsum("blh,bld->hd", mixed, piece, preferred_element_type=jnp.float32)
     rows_grad = jnp.einsum("bld,hd->blh", piece, output_weight, preferred_element_type=jnp.float32)
     output_weight_grad = weight_total

time: 774 us -> 716 us (0.925)
  waiting for transfers between devices: 480 us -> 415 us
  local copies, waits for them, and re-layouts: 25.5 us -> 40.9 us
    reduce_scatter x4, waiting for transfers between devices: 134 us -> 80.6 us  [scatter(): lax.psum_scatter(value, 'dp', scatter_dimension=axis, tiled=True)]
    all_gather x1 -> x0, waiting for transfers between devices: 24.6 us -> none  [shards(): piece = lax.all_gather(attend_grad, 'tensor', axis=0, tiled=True)]
    ppermute x0 -> x3, waiting for transfers between devices: none -> 20.6 us  [the longest x2 15 us: ring_gather(): lax.ppermute(going_up, axis, [(d, (d + 1) % ways) for d in range(ways)])]
    reduce_scatter x4, starting transfers between devices: 11.3 us -> 0.17 us  [scatter(): lax.psum_scatter(value, 'dp', scatter_dimension=axis, tiled=True)]
    unnamed x172 -> x182, local copies, waits for them, and re-layouts: 17.4 us -> 16.9 us
  transfers between devices with their start and end apart: 14 -> 16, of which waited for: 14 -> 15; matrix products, arithmetic and copies ran while one was open for 11% -> 15% of each run, Pallas kernels for 0% -> 0%
where the time goes in v1:
time: 716 us; the launch traced here: 706 us
  waiting for transfers between devices  415 us (58%)
  matrix products  91.2 us (13%)
  blocking collectives  75.5 us (11%)
  other arithmetic  54.3 us (8%)
  local copies, waits for them, and re-layouts  40.9 us (6%)
  between operations  16 us (2%)
  starting transfers between devices  13.1 us (2%)
    reduce_scatter x4, waiting for transfers between devices, scatter(): lax.psum_scatter(value, 'dp', scatter_dimension=axis, tiled=True)  80.6 us
    reduce_scatter x1, waiting for transfers between devices, shards(): lax.psum_scatter(jnp.einsum('blke,dke->bld', piece, project_weight, prefe...  48.2 us
    all_gather x1, waiting for transfers between devices, shards(): lax.all_gather((normed_local * (1.0 + attend_scale) + attend_shift).astyp...  47.1 us
    all_gather x1, waiting for transfers between devices, shards(): mod_two_all = lax.all_gather(mod_two, 'tensor', axis=0, tiled=True)  45.9 us
    reduce_scatter x1, waiting for transfers between devices, shards(): lax.psum_scatter(jnp.einsum('blf,fd->bld', piece, down_weight, preferred_...  45.5 us
    reduce_scatter x1, waiting for transfers between devices, shards(): lax.psum_scatter(jnp.einsum('blh,hd->bld', piece, output_weight, preferre...  45.3 us
    all_gather x1, waiting for transfers between devices, shards(): piece = lax.all_gather(branch_grad, 'tensor', axis=0, tiled=True)  41.2 us
    psum x1, blocking collectives, shards(): small = lax.psum(small, ('dp', 'tensor'))  37.9 us
  transfers between devices with their start and end apart: 16, of which 15 were waited for; matrix products, arithmetic and copies ran while one was open for 15% of the time, Pallas kernels for 0%

profile of v1, /device:TPU:0, one launch (start us, length us, event | category | flops | bytes accessed | tf_op | source)
XLA Modules:
  0.0 706.2 jit_solution(5829355002493686431)
XLA Ops:
  8.1 10.4 %all-gather = s32[8,4,2]{1,2,0:T(2,128)S(1)} all-gather(s32[1,4,2]{1,2,0:T(2,128)S(1)} %add_bitcast_fusion), channel_id=1, replica_groups=mesh['dp'=8,'tensor'=4] {'dp'}, dimensions={0}, use_global_device_ids=true | all-gather | bytes 288 | tf_op jit(solution)/shard_map/all_gather | solution.py:112
  29.4 4.9 all-to-all-start
  34.8 5.1 all-to-all-done
  42.9 47.1 %all-gather.6.cloned.1.call-done = bf16[4,256,1152]{2,1,0:T(8,128)(2,1)} async-done(((bf16[1,256,1152]{2,1,0:T(8,128)(2,1)}), bf16[4,256,1152]{2,1,0:T(8,128)(2,1)}) %all-gather.6.cloned.1.call-update) | async-done | bytes 2359312 | tf_op jit(solution)/shard_map/all_gather | solution.py:140
  90.0 4.7 fusion.10
  107.9 45.3 %reduce-scatter.9.cloned.1.call-done = bf16[1,256,1152]{2,1,0:T(8,128)(2,1)} async-done(((bf16[4,256,1152]{2,1,0:T(8,128)(2,1)}), bf16[1,256,1152]{2,1,0:T(8,128)(2,1)}) %reduce-scatter.9.cloned.1.call-update) | async-done | bytes 589840 | tf_op jit(solution)/shard_map/reduce_scatter | solution.py:164
  160.5 45.9 %all-gather.8.cloned.1.call-done = bf16[4,256,1152]{2,1,0:T(8,128)(2,1)} async-done(((bf16[1,256,1152]{2,1,0:T(8,128)(2,1)}), bf16[4,256,1152]{2,1,0:T(8,128)(2,1)}) %all-gather.8.cloned.1.call-update) | async-done | bytes 2359312 | tf_op jit(solution)/shard_map/all_gather | solution.py:175
  206.4 9.6 %fusion.1 = f32[4,256,2,768]{3,1,2,0:T(8,128)} fusion(bf16[1152,2,768]{2,1,0:T(2,128)(2,1)} %param.30, bf16[4,256,1152]{2,1,0:T(8,128)(2,1)} %all-gather.8.cloned.1.call-done), kind=kOutput, calls=%fused_computation.14 | convolution fusion | flops 3623878656 | bytes 12189696 | tf_op jit(solution)/shard_map/bld,dkf->blkf/dot_general | solution.py:176
  216.0 41.2 %all-gather.10.cloned.1.call-done = bf16[4,256,1152]{2,1,0:T(8,128)(2,1)} async-done(((bf16[1,256,1152]{2,1,0:T(8,128)(2,1)}), bf16[4,256,1152]{2,1,0:T(8,128)(2,1)}) %all-gather.10.cloned.1.call-update) | async-done | bytes 2359312 | tf_op jit(solution)/shard_map/all_gather | solution.py:195
  257.2 8.4 %fusion.26 = (bf16[4,256,1,768]{3,1,0,2:T(8,128)(2,1)S(1)}, bf16[4,256,1,768]{3,1,0,2:T(8,128)(2,1)S(1)}, bf16[4,256,768]{2,1,0:T(8,128)(2,1)}) fusion(f32[4,256,2,768]{3,1,2,0:T(8,128)} %fusion.1, bf16[4,256,1152]{2,1,0:T(8,128)(2,1)} %all-gather.10.cloned.1.call-done, bf16[768,1152]{1,0:T(8,128)(2,1)} %param.31), kind=kOutput, calls=%fused_computation.62 | convolution fusion | flops 1823735808 | bytes 15138816 | tf_op jit(solution)/shard_map/bld,fd->blf/dot_general | solution.py:197
  267.3 5.6 bitcast_convert_fusion.3
  272.9 5.6 convolution_convert_fusion
  278.6 5.4 fusion.4
  285.4 34.1 %reduce-scatter.13.cloned.1.call-done = bf16[1,256,1152]{2,1,0:T(8,128)(2,1)} async-done(((bf16[4,256,1152]{2,1,0:T(8,128)(2,1)}), bf16[1,256,1152]{2,1,0:T(8,128)(2,1)}) %reduce-scatter.13.cloned.1.call-update) | async-done | bytes 589840 | tf_op jit(solution)/shard_map/reduce_scatter | solution.py:207
  323.3 45.5 %reduce-scatter.11.cloned.1.call-done = bf16[1,256,1152]{2,1,0:T(8,128)(2,1)} async-done(((bf16[4,256,1152]{2,1,0:T(8,128)(2,1)}), bf16[1,256,1152]{2,1,0:T(8,128)(2,1)}) %reduce-scatter.11.cloned.1.call-update) | async-done | bytes 589840 | tf_op jit(solution)/shard_map/reduce_scatter | solution.py:183
  368.8 4.3 multiply_reduce_fusion.5
  379.4 5.5 bitcast_convert_fusion
  387.1 6.9 collective-permute-done
  398.9 5.7 collective-permute-done.1
  409.6 8.1 %collective-permute-done.2 = bf16[1,256,1152]{2,1,0:T(8,128)(2,1)} collective-permute-done((bf16[1,256,1152]{2,1,0:T(8,128)(2,1)}, bf16[1,256,1152]{2,1,0:T(8,128)(2,1)}, u32[]{:S(2)}, u32[]{:S(2)}) %collective-permute-start.2) | collective-permute-done | bytes 589856 | tf_op jit(solution)/shard_map/ppermute | solution.py:21
  437.4 4.0 fusion.6
  443.6 3.3 convolution_convert_fusion.3
  447.8 5.3 bitcast_convert_fusion.1
  453.4 6.7 bitcast_convert_fusion.2
  464.5 35.6 %reduce-scatter.19.cloned.1.call-done = bf16[288,144]{0,1:T(8,128)(2,1)} async-done(((bf16[288,1152]{0,1:T(8,128)(2,1)}), bf16[288,144]{0,1:T(8,128)(2,1)}) %reduce-scatter.19.cloned.1.call-update) | async-done | bytes 82960 | tf_op jit(solution)/shard_map/reduce_scatter | solution.py:335
  501.7 44.7 %reduce-scatter.17.cloned.1.call-done = bf16[144,3,288]{2,0,1:T(8,128)(2,1)} async-done(((bf16[1152,3,288]{2,0,1:T(8,128)(2,1)}), bf16[144,3,288]{2,0,1:T(8,128)(2,1)}) %reduce-scatter.17.cloned.1.call-update) | async-done | bytes 248848 | tf_op jit(solution)/shard_map/reduce_scatter | solution.py:335
  548.3 48.2 %reduce-scatter.15.cloned.1.call-done = bf16[1,256,1152]{2,1,0:T(8,128)(2,1)} async-done(((bf16[4,256,1152]{2,1,0:T(8,128)(2,1)}), bf16[1,256,1152]{2,1,0:T(8,128)(2,1)}) %reduce-scatter.15.cloned.1.call-update) | async-done | bytes 589840 | tf_op jit(solution)/shard_map/reduce_scatter | solution.py:259
  600.6 7.7 %reduce.26 = bf16[1152,6]{1,0:T(8,128)(2,1)S(1)} reduce(bf16[1152,1,6]{2,1,0:T(2,128)(2,1)} %bitcast.210, bf16[]{:T(256)} %broadcast.439), dimensions={1}, to_apply=%bitcast.178.reduce_sub_computation | reduce | bytes 27650
  609.3 3.3 all-to-all-start.1
  622.2 18.0 %psum.15 = f32[4,1152]{1,0:T(4,128)S(1)} all-reduce(f32[4,1152]{1,0:T(4,128)S(1)} %convolution_bitcast_fusion.2), channel_id=1, replica_groups=mesh['dp'=8,'tensor'=4] {'tensor'}, use_global_device_ids=true, to_apply=%region_35.36 | all-reduce | flops 4608 | bytes 36864 | tf_op jit(solution)/shard_map/psum | solution.py:289
  641.1 9.2 %all-gather.1 = bf16[8,4,2880]{2,1,0:T(4,128)(2,1)S(1)} all-gather(bf16[1,4,2880]{2,1,0:T(4,128)(2,1)S(1)} %maximum_bitcast_fusion), channel_id=1, replica_groups=mesh['dp'=8,'tensor'=4] {'dp'}, dimensions={0}, use_global_device_ids=true | all-gather | bytes 207360 | tf_op jit(solution)/shard_map/all_gather | solution.py:292
  651.0 37.9 %psum.14 = f32[9360]{0:T(1024)S(1)} all-reduce(f32[9360]{0:T(1024)S(1)} %concatenate.23), channel_id=1, replica_groups=mesh['dp'=8,'tensor'=4] {'dp','tensor'}, use_global_device_ids=true, to_apply=%region_31.32 | all-reduce | flops 9360 | bytes 74880 | tf_op jit(solution)/shard_map/psum | solution.py:326
  (331 shorter events, 117.0 us)
Async XLA Ops:
  7.2 19.0 %copy-start = (bf16[1152,1152]{1,0:T(8,128)(2,1)S(1)}, bf16[1152,1152]{1,0:T(8,128)(2,1)}, u32[]{:S(2)}) copy-start(bf16[1152,1152]{1,0:T(8,128)(2,1)} %param.37) | copy-start | bytes 7962628
  29.4 10.5 %all-to-all-start = ((bf16[4,6,288]{2,1,0:T(8,128)(2,1)}), bf16[4,6,288]{2,1,0:T(8,128)(2,1)S(1)}, u32[]{:S(2)}, u32[]{:S(2)}) async-start(bf16[4,6,288]{2,1,0:T(8,128)(2,1)} %copy.149), calls=%async_computation | async-start | bytes 49152 | tf_op jit(solution)/shard_map/all_to_all | solution.py:132
  34.3 55.7 %all-gather.6.cloned.1.call-start = ((), (), s32[]{:S(2)}) async-start(), calls=%async_computation.10 | async-start | bytes 2949120 | tf_op jit(solution)/shard_map/all_gather | solution.py:140
  34.5 8.0 %copy-start.60 = (f32[256]{0:T(256)}, f32[256]{0:T(256)S(1)}, u32[]{:S(2)}) copy-start(f32[256]{0:T(256)S(1)} %broadcast_multiply_fusion.5) | copy-start | bytes 3076
  34.8 59.9 %copy-start.63 = (f32[256]{0:T(256)}, f32[256]{0:T(256)S(1)}, u32[]{:S(2)}) copy-start(f32[256]{0:T(256)S(1)} %add_rsqrt_fusion.1) | copy-start | bytes 3076
  42.5 110.7 %reduce-scatter.9.cloned.1.call-start = ((), (), s32[]{:S(2)}) async-start(), calls=%async_computation.11 | async-start | bytes 2949120 | tf_op jit(solution)/shard_map/reduce_scatter | solution.py:164
  42.5 52.8 %copy-start.72 = (f32[72]{0:T(128)}, f32[72]{0:T(128)S(1)}, u32[]{:S(2)}) copy-start(f32[72]{0:T(128)S(1)} %convert_element_type.306) | copy-start | bytes 868
  42.6 53.9 %copy-start.70 = (f32[72]{0:T(128)}, f32[72]{0:T(128)S(1)}, u32[]{:S(2)}) copy-start(f32[72]{0:T(128)S(1)} %convert_element_type.309) | copy-start | bytes 868
  106.5 99.9 %all-gather.8.cloned.1.call-start = ((), (), s32[]{:S(2)}) async-start(), calls=%async_computation.12 | async-start | bytes 2949120 | tf_op jit(solution)/shard_map/all_gather | solution.py:175
  156.9 100.3 %all-gather.10.cloned.1.call-start = ((), (), s32[]{:S(2)}) async-start(), calls=%async_computation.14 | async-start | bytes 2949120 | tf_op jit(solution)/shard_map/all_gather | solution.py:195
  160.3 159.2 %reduce-scatter.13.cloned.1.call-start = ((), (), s32[]{:S(2)}) async-start(), calls=%async_computation.15 | async-start | bytes 2949120 | tf_op jit(solution)/shard_map/reduce_scatter | solution.py:207
  257.2 10.1 %copy-start.77 = (bf16[1152,2,768]{2,1,0:T(2,128)(2,1)S(1)}, bf16[1152,2,768]{2,1,0:T(2,128)(2,1)}, u32[]{:S(2)}) copy-start(bf16[1152,2,768]{2,1,0:T(2,128)(2,1)} %param.30) | copy-start | bytes 10616836
  272.9 95.9 %reduce-scatter.11.cloned.1.call-start = ((), (), s32[]{:S(2)}) async-start(), calls=%async_computation.13 | async-start | bytes 2949120 | tf_op jit(solution)/shard_map/reduce_scatter | solution.py:183
  278.5 181.6 %reduce-scatter.23.cloned.1.call-start = ((), (), s32[]{:S(2)}) async-start(), calls=%async_computation.20 | async-start | bytes 1990656 | tf_op jit(solution)/shard_map/reduce_scatter | solution.py:335
  284.0 178.2 %reduce-scatter.21.cloned.1.call-start = ((), (), s32[]{:S(2)}) async-start(), calls=%async_computation.19 | async-start | bytes 3981312 | tf_op jit(solution)/shard_map/reduce_scatter | solution.py:335
  368.8 10.7 %copy-start.79 = (bf16[4,256,1152]{2,1,0:T(8,128)(2,1)S(1)}, bf16[4,256,1152]{2,1,0:T(8,128)(2,1)}, u32[]{:S(2)}) copy-start(bf16[4,256,1152]{2,1,0:T(8,128)(2,1)} %all-gather.8.cloned.1.call-done) | copy-start | bytes 7077892
  368.8 10.7 %copy-start.87 = (bf16[4,256,1,768]{3,1,0,2:T(8,128)(2,1)S(1)}, bf16[4,256,1,768]{3,1,0,2:T(8,128)(2,1)}, u32[]{:S(2)}) copy-start(bf16[4,256,1,768]{3,1,0,2:T(8,128)(2,1)} %copy-done.86) | copy-start | bytes 4718596
  375.6 18.4 %collective-permute-start = (bf16[1,256,1152]{2,1,0:T(8,128)(2,1)}, bf16[1,256,1152]{2,1,0:T(8,128)(2,1)}, u32[]{:S(2)}, u32[]{:S(2)}) collective-permute-start(bf16[1,256,1152]{2,1,0:T(8,128)(2,1)} %get-tuple-element.125), channel_id=1, source_target_pairs={{0,1},{1,2},{2,3},{3,0},{4,5},{5,6},{6,7},{7,4},{8,9},{9,10},{10,1... | collective-permute-start | bytes 1769480 | tf_op jit(solution)/shard_map/ppermute | solution.py:21
  376.4 28.2 %collective-permute-start.1 = (bf16[1,256,1152]{2,1,0:T(8,128)(2,1)}, bf16[1,256,1152]{2,1,0:T(8,128)(2,1)}, u32[]{:S(2)}, u32[]{:S(2)}) collective-permute-start(bf16[1,256,1152]{2,1,0:T(8,128)(2,1)} %get-tuple-element.125), channel_id=1, source_target_pairs={{0,3},{1,0},{2,1},{3,2},{4,7},{5,4},{6,5},{7,6},{8,11},{9,8},{10,9... | collective-permute-start | bytes 1769480 | tf_op jit(solution)/shard_map/ppermute | solution.py:24
  384.9 115.2 %reduce-scatter.19.cloned.1.call-start = ((), (), s32[]{:S(2)}) async-start(), calls=%async_computation.18 | async-start | bytes 995328 | tf_op jit(solution)/shard_map/reduce_scatter | solution.py:335
  387.1 8.9 %copy-start.16 = (bf16[1,256,1152]{1,2,0:T(8,128)(2,1)S(1)}, bf16[1,256,1152]{1,2,0:T(8,128)(2,1)}, u32[]{:S(2)}) copy-start(bf16[1,256,1152]{1,2,0:T(8,128)(2,1)} %copy.158) | copy-start | bytes 1769476
  394.0 23.7 %collective-permute-start.2 = (bf16[1,256,1152]{2,1,0:T(8,128)(2,1)}, bf16[1,256,1152]{2,1,0:T(8,128)(2,1)}, u32[]{:S(2)}, u32[]{:S(2)}) collective-permute-start(bf16[1,256,1152]{2,1,0:T(8,128)(2,1)} %collective-permute-done), channel_id=1, source_target_pairs={{0,1},{1,2},{2,3},{3,0},{4,5},{5,6},{6,7},{7,4},{8,9},{9,10},{10,1... | collective-permute-start | bytes 1769480 | tf_op jit(solution)/shard_map/ppermute | solution.py:21
  441.4 105.0 %reduce-scatter.17.cloned.1.call-start = ((), (), s32[]{:S(2)}) async-start(), calls=%async_computation.17 | async-start | bytes 2985984 | tf_op jit(solution)/shard_map/reduce_scatter | solution.py:335
  453.2 143.3 %reduce-scatter.15.cloned.1.call-start = ((), (), s32[]{:S(2)}) async-start(), calls=%async_computation.16 | async-start | bytes 2949120 | tf_op jit(solution)/shard_map/reduce_scatter | solution.py:259
  462.0 134.5 %copy-start.50 = (f32[1152]{0:T(1024)S(1)}, f32[1152]{0:T(1024)}, u32[]{:S(2)}) copy-start(f32[1152]{0:T(1024)} %copy-done.49) | copy-start | bytes 13828
  462.0 134.5 %copy-start.61 = (f32[256]{0:T(256)S(1)}, f32[256]{0:T(256)}, u32[]{:S(2)}) copy-start(f32[256]{0:T(256)} %copy-done.60) | copy-start | bytes 3076
  462.0 134.5 %copy-start.64 = (f32[256]{0:T(256)S(1)}, f32[256]{0:T(256)}, u32[]{:S(2)}) copy-start(f32[256]{0:T(256)} %copy-done.63) | copy-start | bytes 3076
  609.3 8.8 %all-to-all-start.1 = ((bf16[4,2,864]{2,1,0:T(2,128)(2,1)}), bf16[4,2,864]{2,1,0:T(2,128)(2,1)S(1)}, u32[]{:S(2)}, u32[]{:S(2)}) async-start(bf16[4,2,864]{2,1,0:T(2,128)(2,1)} %reshape.475), calls=%async_computation.6 | async-start | bytes 28672 | tf_op jit(solution)/shard_map/all_to_all | solution.py:282
  622.2 28.7 %copy-start.54 = (f32[1152]{0:T(1024)S(1)}, f32[1152]{0:T(1024)}, u32[]{:S(2)}) copy-start(f32[1152]{0:T(1024)} %get-tuple-element.122) | copy-start | bytes 13828
  622.2 28.7 %copy-start.55 = (f32[1152]{0:T(1024)S(1)}, f32[1152]{0:T(1024)}, u32[]{:S(2)}) copy-start(f32[1152]{0:T(1024)} %get-tuple-element.124) | copy-start | bytes 13828
  622.2 28.7 %copy-start.74 = (f32[72]{0:T(128)S(1)}, f32[72]{0:T(128)}, u32[]{:S(2)}) copy-start(f32[72]{0:T(128)} %get-tuple-element.104) | copy-start | bytes 868
  622.2 28.7 %copy-start.75 = (f32[72]{0:T(128)S(1)}, f32[72]{0:T(128)}, u32[]{:S(2)}) copy-start(f32[72]{0:T(128)} %get-tuple-element.102) | copy-start | bytes 868
  (72 other events, 166.7 us)
Sparse Core Ops, SparseCore 0:
  42.6 47.3 all-gather.5
  106.7 46.4 reduce-scatter.8
  157.0 49.3 all-gather.7
  208.4 48.7 all-gather.9
  273.0 46.4 reduce-scatter.12
  321.7 47.0 reduce-scatter.10
  372.1 38.6 reduce-scatter.22
  414.3 47.8 reduce-scatter.20
  465.5 34.6 reduce-scatter.18
  503.4 42.9 reduce-scatter.16
  548.7 47.7 reduce-scatter.14
